TPU v7x, 32 devices: a whole 2x2x4 slice. The times are simulated.
32 devices in a mesh: ep: 8 (over y, x, core), tp: 4 (over z).
Axes of the slice: x: 2, y: 2, z: 4, core: 2. Of those that a mesh axis runs over, the one named last changes fastest.
Arguments:
- tokens: bfloat16 [512, 7168], P('ep'), may hold values from -6 to 6
- gate_scores: float32 [512, 8], P('ep'), may hold values from 0.1 to 1
- expert_ids: int32 [512, 8], P('ep'), may hold values from 0 to 15, all different within a row; in each aligned block of 64 rows (0 to 63, 64 to 127, ...) at most 48 rows name the same one
- gate_weight: bfloat16 [16, 7168, 2048], P('ep', None, 'tp'), may hold values from -0.0625 to 0.0625
- up_weight: bfloat16 [16, 7168, 2048], P('ep', None, 'tp'), may hold values from -0.0625 to 0.0625
- down_weight: bfloat16 [16, 2048, 7168], P('ep', 'tp'), may hold values from -0.125 to 0.125
Outputs:
- mixed: bfloat16 [512, 7168], P('ep', 'tp')
Inputs may be any that keep to these rules, and one draw needn't show every extreme that they name: `expert_ids`: each row names 8 different experts. Among the tokens of one group, no expert is named by more than 48 tokens, and in every draw some expert is named by exactly 48 of them.
All inputs are finite; a program needn't handle non-finite values.
Results may differ from a plain program's by a relative error of at most 0.02.
Values may be sent and summed in bfloat16 or wider, within the bound.
No kernel may reach another device: no remote copies, remote signals or barrier semaphores. Data moves between devices by JAX's collectives and lax.ppermute only.
A program may use at most 192 MiB of HBM per device.

v0:
```python
import jax
import jax.numpy as jnp
from jax import lax
from jax.sharding import PartitionSpec as P


def local(tokens, gate_scores, expert_ids, gate_weight, up_weight, down_weight):
    n_ep = lax.axis_size("ep")
    n_tp = lax.axis_size("tp")
    tok_count, width = tokens.shape
    choose = expert_ids.shape[1]
    exp_local = gate_weight.shape[0]
    experts = exp_local * n_ep
    capacity = min(tok_count, 3 * tok_count * choose // (2 * experts))
    share = width // n_tp
    expert_range = jnp.arange(experts)
    picked = jnp.sum(
        (expert_ids[:, :, None] == expert_range[None, None, :]).astype(jnp.int32), axis=1
    )
    rank = jnp.cumsum(picked, axis=0) - picked
    slot = jnp.take_along_axis(rank, expert_ids, axis=1)
    token_range = jnp.arange(tok_count)
    slot_range = jnp.arange(capacity)
    hits = (rank.T[:, None, :] == slot_range[None, :, None]) & (picked.T[:, None, :] > 0)
    found = jnp.any(hits, axis=2)
    index = jnp.where(
        found, jnp.sum(hits.astype(jnp.int32) * token_range[None, None, :], axis=2), tok_count
    )
    padded = jnp.concatenate([tokens, jnp.zeros((1, width), jnp.bfloat16)], axis=0)
    outgoing = padded[index].reshape(n_ep, exp_local, capacity, width)
    received = lax.all_to_all(outgoing, "ep", split_axis=0, concat_axis=0, tiled=True)
    gate = jnp.einsum("sjcd,jdf->sjcf", received, gate_weight, preferred_element_type=jnp.float32)
    upper = jnp.einsum("sjcd,jdf->sjcf", received, up_weight, preferred_element_type=jnp.float32)
    hidden = (jax.nn.silu(gate) * upper).astype(jnp.bfloat16)
    partial_value = jnp.einsum(
        "sjcf,jfd->sjcd", hidden, down_weight, preferred_element_type=jnp.float32
    )
    rounded = partial_value.astype(jnp.bfloat16)
    summed = (
        lax.psum_scatter(rounded, "tp", scatter_dimension=3, tiled=True)
        .astype(jnp.float32)
        .astype(jnp.bfloat16)
    )
    returned = lax.all_to_all(summed, "ep", split_axis=0, concat_axis=0, tiled=True)
    results = returned.reshape(experts * capacity, share)
    flat_index = expert_ids * capacity + slot
    chosen_rows = results[flat_index]
    weights = 2.5 * gate_scores / jnp.sum(gate_scores, axis=1, keepdims=True)
    mixed = jnp.einsum("tk,tkd->td", weights, chosen_rows.astype(jnp.float32))
    return mixed.astype(jnp.bfloat16)


def solution(mesh):
    placed = (
        P("ep", None),
        P("ep", None),
        P("ep", None),
        P("ep", None, "tp"),
        P("ep", None, "tp"),
        P("ep", "tp", None),
    )
    return jax.shard_map(
        local, mesh=mesh, in_specs=placed, out_specs=P("ep", "tp"), check_vma=False
    )
```

profile of v0, /device:TPU:0, one launch (start us, length us, event | category | flops | bytes accessed | tf_op | source)
XLA Modules:
  0.0 418.8 jit_solution(12055357871420945862)
XLA Ops:
  6.5 0.7 convert_reduce_fusion
  7.2 0.1 copy.48
  7.3 0.1 reduce_window_sum.11
  7.5 0.4 select_reduce_fusion
  7.9 0.4 fusion.25
  8.3 1.2 concatenate.3
  9.6 9.5 %gather_fusion = bf16[768,7168]{1,0:T(8,128)(2,1)} fusion(bf16[65,7168]{1,0:T(8,128)(2,1)S(1)} %concatenate.3, s32[1024]{0:T(1024)S(1)} %pad_clamp_fusion.1), kind=kCustom, calls=%fused_computation | custom fusion | bytes 22023168 | tf_op jit(solution)/shard_map/gather | solution.py:30
  19.0 127.3 %all_to_all.10 = bf16[8,2,48,7168]{3,2,1,0:T(8,128)(2,1)S(1)} all-to-all(bf16[8,2,48,7168]{3,2,1,0:T(8,128)(2,1)} %bitcast.65), channel_id=1, replica_groups=mesh['ep'=8,'tp'=4] {'ep'}, dimensions={0} | all-to-all | bytes 22020096 | tf_op jit(solution)/shard_map/all_to_all | solution.py:31
  146.3 9.1 %fusion.2 = f32[2,8,48,512]{3,2,1,0:T(8,128)S(1)} fusion(bf16[2,7168,512]{2,1,0:T(8,128)(2,1)} %param.10, bf16[8,2,48,7168]{3,2,1,0:T(8,128)(2,1)S(1)} %all_to_all.10), kind=kOutput, calls=%fused_computation.5 | convolution fusion | flops 5637144576 | bytes 27262976 | tf_op jit(solution)/shard_map/sjcd,jdf->sjcf/dot_general | solution.py:33
  155.4 9.5 %fusion.16 = bf16[8,2,48,512]{3,2,0,1:T(8,128)(2,1)S(1)} fusion(f32[2,8,48,512]{3,2,1,0:T(8,128)S(1)} %fusion.2, bf16[2,7168,512]{2,1,0:T(8,128)(2,1)} %param.9, bf16[8,2,48,7168]{3,2,1,0:T(8,128)(2,1)S(1)} %all_to_all.10), kind=kOutput, calls=%fused_computation.16 | convolution fusion | flops 5639503872 | bytes 28049408 | tf_op jit(solution)/shard_map/sjcd,jdf->sjcf/dot_general | solution.py:32
  165.0 13.9 %fusion.9 = bf16[8,2,48,7168]{3,2,0,1:T(8,128)(2,1)} fusion(bf16[8,2,48,512]{3,2,0,1:T(8,128)(2,1)S(1)} %fusion.16, bf16[2,512,7168]{2,1,0:T(8,128)(2,1)} %param.11), kind=kOutput, calls=%fused_computation.10 | convolution fusion | flops 5642649600 | bytes 26476544 | tf_op jit(solution)/shard_map/sjcf,jfd->sjcd/dot_general | solution.py:35
  178.9 186.2 %reduce-scatter.2.cloned.1.call-done = bf16[8,2,48,1792]{3,2,0,1:T(8,128)(2,1)} async-done(((bf16[8,2,48,7168]{3,2,0,1:T(8,128)(2,1)}), bf16[8,2,48,1792]{3,2,0,1:T(8,128)(2,1)}) %reduce-scatter.2.cloned.1.call-update) | async-done | bytes 2752528 | tf_op jit(solution)/shard_map/reduce_scatter | solution.py:40
  365.1 3.5 copy.53
  368.6 3.7 all-to-all-start.1
  372.3 0.1 copy.54
  372.4 0.1 reshape.61
  372.5 3.8 gather_fusion.2
  376.4 0.1 copy.56
  376.5 0.1 reshape.55
  376.6 0.1 copy.60
  376.8 29.1 %all-to-all-done.1 = bf16[8,2,48,1792]{3,2,1,0:T(8,128)(2,1)S(1)} async-done(((bf16[8,2,48,1792]{3,2,1,0:T(8,128)(2,1)}), bf16[8,2,48,1792]{3,2,1,0:T(8,128)(2,1)S(1)}, u32[]{:S(2)}, u32[]{:S(2)}) %all-to-all-start.1) | async-done | bytes 2752544 | tf_op jit(solution)/shard_map/all_to_all | solution.py:44
  405.9 3.2 gather_fusion.1
  409.1 2.1 fusion.14
  411.2 0.7 copy.69
  (19 shorter events, 0.4 us)
Async XLA Ops:
  6.5 358.5 %reduce-scatter.2.cloned.1.call-start = ((), (), s32[]{:S(2)}) async-start(), calls=%async_computation.3 | async-start | bytes 13762560 | tf_op jit(solution)/shard_map/reduce_scatter | solution.py:40
  178.9 193.4 %copy-start = (s32[64,8]{0,1:T(8,128)S(1)}, s32[64,8]{0,1:T(8,128)}, u32[]{:S(2)}) copy-start(s32[64,8]{0,1:T(8,128)} %param.8) | copy-start | bytes 6148
  368.6 37.3 %all-to-all-start.1 = ((bf16[8,2,48,1792]{3,2,1,0:T(8,128)(2,1)}), bf16[8,2,48,1792]{3,2,1,0:T(8,128)(2,1)S(1)}, u32[]{:S(2)}, u32[]{:S(2)}) async-start(bf16[8,2,48,1792]{3,2,1,0:T(8,128)(2,1)} %copy.53), calls=%async_computation.2 | async-start | bytes 5505024 | tf_op jit(solution)/shard_map/all_to_all | solution.py:44
  372.5 4.1 copy-start.1
Sparse Core Ops, SparseCore 0:
  179.0 186.0 reduce-scatter.1
where the time goes:
time: 419 us
  waiting for transfers between devices  215 us (51%)
  blocking collectives  127 us (30%)
  matrix products  34.7 us (8%)
  local copies, waits for them, and re-layouts  22.7 us (5%)
  between operations  13.5 us (3%)
    reduce_scatter x1, waiting for transfers between devices, local(): lax.psum_scatter(rounded, 'tp', scatter_dimension=3, tiled=True)  186 us
    all_to_all x1, blocking collectives, local(): lax.all_to_all(outgoing, 'ep', split_axis=0, concat_axis=0, tiled=True)  127 us
    all_to_all x1, waiting for transfers between devices, local(): lax.all_to_all(summed, 'ep', split_axis=0, concat_axis=0, tiled=True)  29.1 us
    dot_general x1, matrix products, local(): jnp.einsum('sjcf,jfd->sjcd', hidden, down_weight, preferred_element_type=...  13.9 us
    dot_general x1, matrix products, local(): jnp.einsum('sjcd,jdf->sjcf', received, gate_weight, preferred_element_typ...  9.55 us
    gather x1, local copies, waits for them, and re-layouts, local(): outgoing = padded[index].reshape(n_ep, exp_local, capacity, width)  9.46 us
    dot_general x1, matrix products, local(): jnp.einsum('sjcd,jdf->sjcf', received, up_weight, preferred_element_type=...  9.1 us
  transfers between devices with their start and end apart: 2, of which 2 were waited for; matrix products, arithmetic and copies ran while one was open for 1% of the time, Pallas kernels for 0%

commit v1 on v0

--- a/solution.py
+++ b/solution.py
@@ -41,7 +41,15 @@
         .astype(jnp.float32)
         .astype(jnp.bfloat16)
     )
-    returned = lax.all_to_all(summed, "ep", split_axis=0, concat_axis=0, tiled=True)
+    ways, here = (lax.axis_size("ep"), lax.axis_index("ep"))
+    width_2 = summed.shape[0] // ways
+    turned = jnp.roll(summed, -here * width_2, axis=0)
+    got = [lax.slice_in_dim(turned, 0, width_2, axis=0)]
+    for far in range(1, ways):
+        sent = lax.slice_in_dim(turned, far * width_2, (far + 1) * width_2, axis=0)
+        got.append(lax.ppermute(sent, "ep", [(d, (d + far) % ways) for d in range(ways)]))
+    line = jnp.concatenate(got[::-1], axis=0)
+    returned = jnp.roll(line, (here + 1) * got[0].shape[0], axis=0)
     results = returned.reshape(experts * capacity, share)
     flat_index = expert_ids * capacity + slot
     chosen_rows = results[flat_index]

time: 419 us -> 423 us (level)
  other arithmetic: 1.6 us -> 6.04 us
    ppermute x0 -> x7, waiting for transfers between devices: none -> 31 us  [local(): lax.ppermute(sent, 'ep', [(d, (d + far) % ways) for d in range(ways)])]
    all_to_all x1 -> x0, waiting for transfers between devices: 29.1 us -> none  [local(): lax.all_to_all(summed, 'ep', split_axis=0, concat_axis=0, tiled=True)]
    ppermute x0 -> x7, starting transfers between devices: none -> 4.46 us  [local(): lax.ppermute(sent, 'ep', [(d, (d + far) % ways) for d in range(ways)])]
  transfers between devices with their start and end apart: 2 -> 8, of which waited for: 2 -> 6; matrix products, arithmetic and copies ran while one was open for 1% -> 0% of each run, Pallas kernels for 0% -> 0%
where the time goes in v1:
time: 423 us
  waiting for transfers between devices  217 us (51%)
  blocking collectives  127 us (30%)
  matrix products  34.7 us (8%)
  local copies, waits for them, and re-layouts  19.9 us (5%)
  between operations  13.6 us (3%)
  other arithmetic  6.04 us (1%)
  starting transfers between devices  4.46 us (1%)
    reduce_scatter x1, waiting for transfers between devices, local(): lax.psum_scatter(rounded, 'tp', scatter_dimension=3, tiled=True)  186 us
    all_to_all x1, blocking collectives, local(): lax.all_to_all(outgoing, 'ep', split_axis=0, concat_axis=0, tiled=True)  127 us
    ppermute x7, waiting for transfers between devices, local(): lax.ppermute(sent, 'ep', [(d, (d + far) % ways) for d in range(ways)])  31 us
    dot_general x1, matrix products, local(): jnp.einsum('sjcf,jfd->sjcd', hidden, down_weight, preferred_element_type=...  13.9 us
    dot_general x1, matrix products, local(): jnp.einsum('sjcd,jdf->sjcf', received, gate_weight, preferred_element_typ...  9.55 us
    gather x1, local copies, waits for them, and re-layouts, local(): outgoing = padded[index].reshape(n_ep, exp_local, capacity, width)  9.46 us
    dot_general x1, matrix products, local(): jnp.einsum('sjcd,jdf->sjcf', received, up_weight, preferred_element_type=...  9.1 us
  transfers between devices with their start and end apart: 8, of which 6 were waited for; matrix products, arithmetic and copies ran while one was open for 0% of the time, Pallas kernels for 0%

profile of v1, /device:TPU:0, one launch (start us, length us, event | category | flops | bytes accessed | tf_op | source)
XLA Modules:
  0.0 423.1 jit_solution(13823642466320991756)
XLA Ops:
  6.5 0.7 convert_reduce_fusion
  7.9 0.4 fusion.27
  8.2 0.7 bitcast_or_fusion
  9.2 3.8 gather_fusion.2
  13.4 9.5 %gather_fusion = bf16[768,7168]{1,0:T(8,128)(2,1)} fusion(bf16[65,7168]{1,0:T(8,128)(2,1)S(1)} %concatenate.9, s32[1024]{0:T(1024)S(1)} %get-tuple-element.14), kind=kCustom, calls=%fused_computation | custom fusion | bytes 22023168 | tf_op jit(solution)/shard_map/gather | solution.py:30
  22.9 127.3 %all_to_all.5 = bf16[8,2,48,7168]{3,2,1,0:T(8,128)(2,1)S(1)} all-to-all(bf16[8,2,48,7168]{3,2,1,0:T(8,128)(2,1)} %bitcast.65), channel_id=1, replica_groups=mesh['ep'=8,'tp'=4] {'ep'}, dimensions={0} | all-to-all | bytes 22020096 | tf_op jit(solution)/shard_map/all_to_all | solution.py:31
  150.2 9.1 %fusion.2 = f32[2,8,48,512]{3,2,1,0:T(8,128)S(1)} fusion(bf16[2,7168,512]{2,1,0:T(8,128)(2,1)} %param.12, bf16[8,2,48,7168]{3,2,1,0:T(8,128)(2,1)S(1)} %all_to_all.5), kind=kOutput, calls=%fused_computation.5 | convolution fusion | flops 5637144576 | bytes 27262976 | tf_op jit(solution)/shard_map/sjcd,jdf->sjcf/dot_general | solution.py:33
  159.3 9.5 %fusion.18 = bf16[8,2,48,512]{3,2,0,1:T(8,128)(2,1)S(1)} fusion(f32[2,8,48,512]{3,2,1,0:T(8,128)S(1)} %fusion.2, bf16[2,7168,512]{2,1,0:T(8,128)(2,1)} %param.11, bf16[8,2,48,7168]{3,2,1,0:T(8,128)(2,1)S(1)} %all_to_all.5), kind=kOutput, calls=%fused_computation.22 | convolution fusion | flops 5639503872 | bytes 28049408 | tf_op jit(solution)/shard_map/sjcd,jdf->sjcf/dot_general | solution.py:32
  168.8 13.9 %fusion.9 = bf16[8,2,48,7168]{3,2,0,1:T(8,128)(2,1)} fusion(bf16[8,2,48,512]{3,2,0,1:T(8,128)(2,1)S(1)} %fusion.18, bf16[2,512,7168]{2,1,0:T(8,128)(2,1)} %param.13), kind=kOutput, calls=%fused_computation.10 | convolution fusion | flops 5642649600 | bytes 26476544 | tf_op jit(solution)/shard_map/sjcf,jfd->sjcd/dot_general | solution.py:35
  182.8 186.2 %reduce-scatter.2.cloned.1.call-done = bf16[8,2,48,1792]{3,2,0,1:T(8,128)(2,1)} async-done(((bf16[8,2,48,7168]{3,2,0,1:T(8,128)(2,1)}), bf16[8,2,48,1792]{3,2,0,1:T(8,128)(2,1)}) %reduce-scatter.2.cloned.1.call-update) | async-done | bytes 2752528 | tf_op jit(solution)/shard_map/reduce_scatter | solution.py:40
  368.9 2.8 fusion.15
  371.7 1.5 fusion.28
  373.2 1.8 collective-permute-start
  375.0 0.7 collective-permute-start.1
  375.8 0.4 collective-permute-start.2
  376.1 1.5 collective-permute-start.3
  377.8 5.8 %collective-permute-done = bf16[1,2,48,1792]{3,2,0,1:T(8,128)(2,1)S(1)} collective-permute-done((bf16[1,2,48,1792]{3,2,0,1:T(8,128)(2,1)}, bf16[1,2,48,1792]{3,2,0,1:T(8,128)(2,1)S(1)}, u32[]{:S(2)}, u32[]{:S(2)}) %collective-permute-start) | collective-permute-done | bytes 344096 | tf_op jit(solution)/shard_map/ppermute | solution.py:50
  383.6 7.3 %collective-permute-done.1 = bf16[1,2,48,1792]{3,2,0,1:T(8,128)(2,1)S(1)} collective-permute-done((bf16[1,2,48,1792]{3,2,0,1:T(8,128)(2,1)}, bf16[1,2,48,1792]{3,2,0,1:T(8,128)(2,1)S(1)}, u32[]{:S(2)}, u32[]{:S(2)}) %collective-permute-start.1) | collective-permute-done | bytes 344096 | tf_op jit(solution)/shard_map/ppermute | solution.py:50
  391.3 16.9 %collective-permute-done.3 = bf16[1,2,48,1792]{3,2,0,1:T(8,128)(2,1)S(1)} collective-permute-done((bf16[1,2,48,1792]{3,2,0,1:T(8,128)(2,1)}, bf16[1,2,48,1792]{3,2,0,1:T(8,128)(2,1)S(1)}, u32[]{:S(2)}, u32[]{:S(2)}) %collective-permute-start.3) | collective-permute-done | bytes 344096 | tf_op jit(solution)/shard_map/ppermute | solution.py:50
  408.3 0.6 collective-permute-done.4
  409.1 1.0 fusion.14
  410.3 3.2 gather_fusion.1
  413.5 2.1 fusion.16
  415.6 0.7 copy.69
  (43 shorter events, 2.3 us)
Async XLA Ops:
  6.5 362.4 %reduce-scatter.2.cloned.1.call-start = ((), (), s32[]{:S(2)}) async-start(), calls=%async_computation.2 | async-start | bytes 13762560 | tf_op jit(solution)/shard_map/reduce_scatter | solution.py:40
  9.2 4.0 copy-start.1
  9.2 4.2 copy-start
  371.7 3.3 copy-start.2
  373.2 10.4 %collective-permute-start = (bf16[1,2,48,1792]{3,2,0,1:T(8,128)(2,1)}, bf16[1,2,48,1792]{3,2,0,1:T(8,128)(2,1)S(1)}, u32[]{:S(2)}, u32[]{:S(2)}) collective-permute-start(bf16[1,2,48,1792]{3,2,0,1:T(8,128)(2,1)} %get-tuple-element.12), channel_id=1, source_target_pairs={{0,28},{4,0},{8,4},{12,8},{16,12},{20,16},{24,20},{28,24},{1,29},{... | collective-permute-start | bytes 1032200 | tf_op jit(solution)/shard_map/ppermute | solution.py:50
  375.0 15.9 %collective-permute-start.1 = (bf16[1,2,48,1792]{3,2,0,1:T(8,128)(2,1)}, bf16[1,2,48,1792]{3,2,0,1:T(8,128)(2,1)S(1)}, u32[]{:S(2)}, u32[]{:S(2)}) collective-permute-start(bf16[1,2,48,1792]{3,2,0,1:T(8,128)(2,1)} %get-tuple-element.11), channel_id=1, source_target_pairs={{0,24},{4,28},{8,0},{12,4},{16,8},{20,12},{24,16},{28,20},{1,25},{... | collective-permute-start | bytes 1032200 | tf_op jit(solution)/shard_map/ppermute | solution.py:50
  375.8 15.5 %collective-permute-start.2 = (bf16[1,2,48,1792]{3,2,0,1:T(8,128)(2,1)}, bf16[1,2,48,1792]{3,2,0,1:T(8,128)(2,1)S(1)}, u32[]{:S(2)}, u32[]{:S(2)}) collective-permute-start(bf16[1,2,48,1792]{3,2,0,1:T(8,128)(2,1)} %get-tuple-element.10), channel_id=1, source_target_pairs={{0,20},{4,24},{8,28},{12,0},{16,4},{20,8},{24,12},{28,16},{1,21},{... | collective-permute-start | bytes 1032200 | tf_op jit(solution)/shard_map/ppermute | solution.py:50
  376.1 32.1 %collective-permute-start.3 = (bf16[1,2,48,1792]{3,2,0,1:T(8,128)(2,1)}, bf16[1,2,48,1792]{3,2,0,1:T(8,128)(2,1)S(1)}, u32[]{:S(2)}, u32[]{:S(2)}) collective-permute-start(bf16[1,2,48,1792]{3,2,0,1:T(8,128)(2,1)} %get-tuple-element.9), channel_id=1, source_target_pairs={{0,16},{4,20},{8,24},{12,28},{16,0},{20,4},{24,8},{28,12},{1,17},{... | collective-permute-start | bytes 1032200 | tf_op jit(solution)/shard_map/ppermute | solution.py:50
  377.7 31.2 %collective-permute-start.4 = (bf16[1,2,48,1792]{3,2,0,1:T(8,128)(2,1)}, bf16[1,2,48,1792]{3,2,0,1:T(8,128)(2,1)S(1)}, u32[]{:S(2)}, u32[]{:S(2)}) collective-permute-start(bf16[1,2,48,1792]{3,2,0,1:T(8,128)(2,1)} %get-tuple-element.8), channel_id=1, source_target_pairs={{0,12},{4,16},{8,20},{12,24},{16,28},{20,0},{24,4},{28,8},{1,13},{... | collective-permute-start | bytes 1032200 | tf_op jit(solution)/shard_map/ppermute | solution.py:50
  383.5 25.4 %collective-permute-start.5 = (bf16[1,2,48,1792]{3,2,0,1:T(8,128)(2,1)}, bf16[1,2,48,1792]{3,2,0,1:T(8,128)(2,1)S(1)}, u32[]{:S(2)}, u32[]{:S(2)}) collective-permute-start(bf16[1,2,48,1792]{3,2,0,1:T(8,128)(2,1)} %get-tuple-element.7), channel_id=1, source_target_pairs={{0,8},{4,12},{8,16},{12,20},{16,24},{20,28},{24,0},{28,4},{1,9},{5... | collective-permute-start | bytes 1032200 | tf_op jit(solution)/shard_map/ppermute | solution.py:50
  390.9 18.1 %collective-permute-start.6 = (bf16[1,2,48,1792]{3,2,0,1:T(8,128)(2,1)}, bf16[1,2,48,1792]{3,2,0,1:T(8,128)(2,1)S(1)}, u32[]{:S(2)}, u32[]{:S(2)}) collective-permute-start(bf16[1,2,48,1792]{3,2,0,1:T(8,128)(2,1)} %get-tuple-element.6), channel_id=1, source_target_pairs={{0,4},{4,8},{8,12},{12,16},{16,20},{20,24},{24,28},{28,0},{1,5},{5... | collective-permute-start | bytes 1032200 | tf_op jit(solution)/shard_map/ppermute | solution.py:50
Sparse Core Ops, SparseCore 0:
  182.9 186.0 reduce-scatter.1
